TPU v7x, 64 devices: a 2x2x8 block of a 4x4x8 slice. The times are simulated.
64 devices in a mesh: rep: 4 (over x, y), dp: 16 (over z, core).
Axes of the slice: x: 2, y: 2, z: 8, core: 2. Of those that a mesh axis runs over, the one named last changes fastest.
The devices are a block of a 4x4x8 slice.
Arguments:
- x: bfloat16 [64, 2048, 640], P(('rep', 'dp')), parts along dimension 0
- dy: bfloat16 [64, 2048, 640], P(('rep', 'dp')), parts along dimension 0
- w_gate: bfloat16 [2, 640, 2048], replicated
- w_up: bfloat16 [2, 640, 2048], replicated
- w_down: bfloat16 [2, 2048, 640], replicated
- m_w_gate: float32 [2, 640, 2048], replicated
- m_w_up: float32 [2, 640, 2048], replicated
- m_w_down: float32 [2, 2048, 640], replicated
- v_w_gate: float32 [2, 640, 2048], replicated
- v_w_up: float32 [2, 640, 2048], replicated
- v_w_down: float32 [2, 2048, 640], replicated
Outputs:
- output 1: bfloat16 [8, 640, 2048], P('rep'), parts along dimension 0
- output 2: bfloat16 [8, 640, 2048], P('rep'), parts along dimension 0
- output 3: bfloat16 [8, 2048, 640], P('rep'), parts along dimension 0
- output 4: float32 [8, 640, 2048], P('rep'), parts along dimension 0
- output 5: float32 [8, 640, 2048], P('rep'), parts along dimension 0
- output 6: float32 [8, 2048, 640], P('rep'), parts along dimension 0
- output 7: float32 [8, 640, 2048], P('rep'), parts along dimension 0
- output 8: float32 [8, 640, 2048], P('rep'), parts along dimension 0
- output 9: float32 [8, 2048, 640], P('rep'), parts along dimension 0
There are 4 independent parts. A program takes and returns all parts, laid end to end along the dimension named above; an argument that names none is the same for every part.
All inputs are finite; a program needn't handle non-finite values.
Results may differ from a plain program's by a relative error of at most 0.0226.
Values are sent between devices in bfloat16 or wider.
A program may use at most 768 MiB of HBM per device.

v0:
```python
import jax
import jax.numpy as jnp
from jax import lax
from jax.sharding import PartitionSpec as P

NAMES = ("w_gate", "w_up", "w_down")


def matmul(a, w):
    return jnp.dot(a, w, preferred_element_type=jnp.float32).astype(jnp.bfloat16)


def normed(h):
    wide = h.astype(jnp.float32)
    scale = lax.rsqrt(jnp.mean(wide**2, -1, keepdims=True) + 1e-6)
    return (wide * scale).astype(jnp.bfloat16)


def layer(h, w):
    a = normed(h)
    gate = jnp.dot(a, w["w_gate"], preferred_element_type=jnp.float32)
    up = jnp.dot(a, w["w_up"], preferred_element_type=jnp.float32)
    return h + matmul((jax.nn.silu(gate) * up).astype(jnp.bfloat16), w["w_down"])


def adamw(w, m, v, g):
    m = 0.9 * m + 0.1 * g
    v = 0.95 * v + 0.05 * g * g
    step = m * lax.rsqrt(v + 1e-8) + 0.1 * w
    return (w - 0.02 * step).astype(jnp.bfloat16), m, v


def clipped(gradients, sum_of_squares, count):
    factor = jnp.minimum(1.0, 0.5 * lax.rsqrt(sum_of_squares / count + 1e-30))
    return [g * factor for g in gradients]


def solution(mesh):
    def step(x, dy, *arrays):
        weights, m, v = (arrays[i : i + 3] for i in (0, 3, 6))
        layers = weights[0].shape[0]
        h, kept = x[0], []
        for number in range(layers):
            kept.append(h)
            h = layer(h, {name: w[number] for name, w in zip(NAMES, weights, strict=True)})
        by_h, summed = dy[0], [None] * layers
        for number in reversed(range(layers)):
            _, back = jax.vjp(lambda w, h: layer(h, w), {name: w[number] for name, w in zip(NAMES, weights, strict=True)}, kept[number])
            by_w, by_h = back(by_h)
            summed[number] = [lax.psum(by_w[name], "dp") for name in NAMES]
        gradients = [jnp.stack([summed[number][i] for number in range(layers)]).astype(jnp.float32) for i in range(3)]
        gradients = clipped(gradients, sum(jnp.sum(g * g) for g in gradients), sum(g.size for g in gradients))
        new = [adamw(w.astype(jnp.float32), m, v, g) for w, m, v, g in zip(weights, m, v, gradients, strict=True)]
        return tuple(one[which] for which in range(3) for one in new)

    return jax.shard_map(
        step,
        mesh=mesh,
        in_specs=(P(("rep", "dp"), None, None),) * 2 + (P(None, None, None),) * 9,
        out_specs=(P("rep", None, None),) * 9,
        check_vma=False,
    )
```

profile of v0, /device:TPU:21, one launch (start us, length us, event | category | flops | bytes accessed | tf_op | source)
XLA Modules:
  0.0 487.6 jit_solution(17178705646663566991)
XLA Ops:
  7.2 0.1 all-reduce.3.cloned.1.call-start
  7.3 3.0 copy.20
  10.3 0.0 copy-start.2
  10.3 0.6 fusion.36
  10.8 0.0 copy-start.11
  10.8 4.7 copy.21
  15.6 0.0 copy-start.8
  15.6 11.3 %convolution_convert_fusion.1 = bf16[2048,2048]{1,0:T(8,128)(2,1)} fusion(bf16[1,2048,640]{2,1,0:T(8,128)(2,1)} %param.12, bf16[2,2048,640]{2,1,0:T(8,128)(2,1)} %param.15), kind=kOutput, calls=%fused_computation.65 | convolution fusion | flops 5372903424 | bytes 13631488 | tf_op jit(solution)/shard_map/transpose(jvp())/dot_general | solution.py:10
  26.8 0.0 copy-done.8
  26.8 11.6 %fusion.74 = f32[2048,2048]{1,0:T(8,128)} fusion(bf16[2,640,2048]{2,1,0:T(8,128)(2,1)} %param.13, bf16[1,2048,640]{2,1,0:T(8,128)(2,1)S(1)} %copy-done.8, f32[2048]{0:T(1024)S(1)} %add_rsqrt_fusion), kind=kOutput, calls=%fused_computation.110 | convolution fusion | flops 5372641280 | bytes 22028288 | tf_op jit(solution)/shard_map/dot_general | solution.py:21
  38.4 0.0 copy-done.11
  38.4 16.9 %multiply_convert_fusion.1 = (bf16[2048,2048]{1,0:T(8,128)(2,1)}, f32[2048,2048]{1,0:T(8,128)}) fusion(f32[2048,2048]{1,0:T(8,128)} %fusion.74, bf16[2,640,2048]{2,1,0:T(8,128)(2,1)} %param.14, bf16[1,2048,640]{2,1,0:T(8,128)(2,1)} %param.11, f32[2048]{0:T(1024)S(1)} %add_rsqrt_fusion), kind=kOutput, calls=%fused_computation.17 | convolution fusion | flops 5397807104 | bytes 47194112 | tf_op jit(solution)/shard_map/dot_general | solution.py:22
  55.3 0.0 copy-done.2
  55.3 9.2 %fusion.40 = (f32[2048]{0:T(1024)S(1)}, bf16[2048,640]{0,1:T(8,128)(2,1)S(1)}) fusion(bf16[2048,2048]{1,0:T(8,128)(2,1)} %get-tuple-element.24, bf16[2,2048,640]{2,1,0:T(8,128)(2,1)} %param.15, bf16[1,2048,640]{1,2,0:T(8,128)(2,1)S(1)} %copy.20), kind=kOutput, calls=%fused_computation.73 | convolution fusion | flops 5375260672 | bytes 16261120 | tf_op jit(solution)/shard_map/dot_general | solution.py:10
  64.5 0.0 copy-start.6
  64.5 0.0 copy-start.9
  64.5 1.5 copy-done.6
  66.0 0.0 copy-done.9
  66.0 12.2 %fusion.63 = f32[2048,2048]{1,0:T(8,128)} fusion(bf16[2,640,2048]{2,1,0:T(8,128)(2,1)} %param.14, bf16[2048,640]{0,1:T(8,128)(2,1)S(1)} %get-tuple-element.27, f32[2048]{0:T(1024)S(1)} %fusion.98), kind=kOutput, calls=%fused_computation.99 | convolution fusion | flops 5372641280 | bytes 22028288 | tf_op jit(solution)/shard_map/jvp()/dot_general | solution.py:22
  78.2 0.0 slice-start.2
  78.2 25.1 %fusion.2 = (bf16[2048,2048]{1,0:T(8,128)(2,1)}, f32[2048,2048]{1,0:T(8,128)}) fusion(f32[2048,2048]{1,0:T(8,128)} %fusion.63, bf16[2048,2048]{1,0:T(8,128)(2,1)} %convolution_convert_fusion.1, bf16[2,640,2048]{2,1,0:T(8,128)(2,1)} %param.13, bf16[2048,640]{0,1:T(8,128)(2,1)} %copy-done.6, f32[2048]{0:T(1024)S(1)} %fusion.98), kind=kOutput, calls=%fused_computation.8 | convolution fusion | flops 5422972928 | bytes 55582720 | tf_op jit(solution)/shard_map/jvp()/dot_general | solution.py:21
  103.3 0.0 slice-start.3
  103.3 16.9 %fusion.55 = bf16[1,2048,640]{2,1,0:T(8,128)(2,1)} fusion(f32[2048,2048]{1,0:T(8,128)} %fusion.63, bf16[1,2048,640]{2,1,0:T(8,128)(2,1)} %param.12, f32[2048,2048]{1,0:T(8,128)} %get-tuple-element.29), kind=kOutput, calls=%fused_computation.91 | convolution fusion | flops 5395185664 | bytes 38797312 | tf_op jit(solution)/shard_map/transpose(jvp())/dot_general | solution.py:10
  120.2 0.0 slice-start
  120.2 13.3 %fusion.58 = bf16[1,640,2048]{2,1,0:T(8,128)(2,1)} fusion(bf16[2048,2048]{1,0:T(8,128)(2,1)} %convolution_convert_fusion.1, bf16[2048,640]{0,1:T(8,128)(2,1)} %copy-done.6, f32[2048]{0:T(1024)S(1)} %fusion.98, f32[2048,2048]{1,0:T(8,128)} %get-tuple-element.29), kind=kOutput, calls=%fused_computation.94 | convolution fusion | flops 5399117824 | bytes 30416896 | tf_op jit(solution)/shard_map/transpose(jvp())/dot_general | solution.py:22
  133.5 0.0 slice-done.2
  133.5 0.0 slice-done.3
  133.5 0.0 slice-start.1
  133.5 12.4 %fusion.44 = bf16[2048,640]{0,1:T(8,128)(2,1)} fusion(bf16[2048,2048]{1,0:T(8,128)(2,1)} %convolution_convert_fusion.1, bf16[2,640,2048]{2,1,0:T(8,128)(2,1)S(1)} %bitcast.77, f32[2048,2048]{1,0:T(8,128)} %get-tuple-element.29), kind=kOutput, calls=%fused_computation.81 | convolution fusion | flops 5395185664 | bytes 30408704 | tf_op jit(solution)/shard_map/transpose(jvp())/dot_general | solution.py:22
  145.9 0.0 copy-start.7
  145.9 10.9 %fusion.56 = bf16[1,640,2048]{2,1,0:T(8,128)(2,1)} fusion(bf16[2048,2048]{1,0:T(8,128)(2,1)} %get-tuple-element.28, bf16[2048,640]{0,1:T(8,128)(2,1)} %copy-done.6, f32[2048]{0:T(1024)S(1)} %fusion.98), kind=kOutput, calls=%fused_computation.92 | convolution fusion | flops 5372641280 | bytes 13639680 | tf_op jit(solution)/shard_map/transpose(jvp())/dot_general | solution.py:21
  156.9 0.0 slice-done
  156.9 0.0 slice-done.1
  156.9 0.0 copy-done.7
  156.9 0.0 copy-done.14
  156.9 0.0 copy-start.10
  156.9 0.0 copy-start.1
  156.9 8.5 %fusion.42 = (f32[2048]{0:T(1024)S(1)}, bf16[2048,640]{0,1:T(8,128)(2,1)S(1)}) fusion(bf16[2048,640]{0,1:T(8,128)(2,1)S(1)} %copy-done.7, bf16[2048,640]{0,1:T(8,128)(2,1)S(1)} %copy-done.14, bf16[2048,2048]{1,0:T(8,128)(2,1)} %get-tuple-element.28, bf16[2,640,2048]{2,1,0:T(8,128)(2,1)S(1)} %bitcast.75), kind=kOutput, calls=%fused_computation.75 | convolution fusion | flops 5375260672 | bytes 18882560 | tf_op jit(solution)/shard_map/transpose(jvp())/dot_general | solution.py:21
  165.4 0.0 copy-done.10
  165.4 0.0 copy-done.1
  165.4 0.0 slice-start.4
  165.4 2.0 fusion.60
  167.5 0.0 slice-start.5
  167.5 10.5 %fusion.57 = bf16[1,2048,640]{2,1,0:T(8,128)(2,1)} fusion(bf16[2048,2048]{1,0:T(8,128)(2,1)} %get-tuple-element.24, bf16[2048,640]{0,1:T(8,128)(2,1)S(1)} %fusion.60), kind=kOutput, calls=%fused_computation.93 | convolution fusion | flops 5370019840 | bytes 13631488 | tf_op jit(solution)/shard_map/transpose(jvp())/dot_general | solution.py:10
  178.0 0.0 slice-done.4
  178.0 0.0 slice-done.5
  178.0 0.0 copy-start.12
  178.0 7.3 %convolution_convert_fusion = bf16[2048,2048]{1,0:T(8,128)(2,1)S(1)} fusion(bf16[2048,640]{0,1:T(8,128)(2,1)S(1)} %fusion.60, bf16[2,2048,640]{2,1,0:T(8,128)(2,1)S(1)} %bitcast.79), kind=kOutput, calls=%fused_computation.64 | convolution fusion | flops 5372903424 | bytes 13631488 | tf_op jit(solution)/shard_map/transpose(jvp())/dot_general | solution.py:10
  185.3 0.0 copy-done.3
  185.3 0.0 copy-done.12
  185.3 0.0 copy-start.13
  185.3 13.9 %fusion.51 = bf16[1,640,2048]{2,1,0:T(8,128)(2,1)} fusion(bf16[2048,2048]{1,0:T(8,128)(2,1)S(1)} %convolution_convert_fusion, f32[2048,2048]{1,0:T(8,128)} %fusion.74, bf16[1,2048,640]{1,2,0:T(8,128)(2,1)S(1)} %copy-done.3, f32[2048]{0:T(1024)S(1)} %copy-done.12), kind=kOutput, calls=%fused_computation.89 | convolution fusion | flops 5399117824 | bytes 30416896 | tf_op jit(solution)/shard_map/transpose(jvp())/dot_general | solution.py:22
  199.2 0.0 copy-done.13
  199.2 19.2 %fusion.52 = bf16[1,640,2048]{2,1,0:T(8,128)(2,1)} fusion(f32[2048,2048]{1,0:T(8,128)} %fusion.74, f32[2048,2048]{1,0:T(8,128)} %get-tuple-element.25, bf16[2048,2048]{1,0:T(8,128)(2,1)} %copy-done.13, bf16[1,2048,640]{1,2,0:T(8,128)(2,1)S(1)} %copy-done.3, f32[2048]{0:T(1024)S(1)} %copy-done.12), kind=kOutput, calls=%fused_computation.90 | convolution fusion | flops 5420089344 | bytes 47194112 | tf_op jit(solution)/shard_map/transpose(jvp())/dot_general | solution.py:21
  218.5 0.1 all-reduce.3.cloned.1.call-update
  218.5 187.0 %all-reduce.3.cloned.1.call-done = (bf16[1,640,2048]{2,1,0:T(8,128)(2,1)}, bf16[1,640,2048]{2,1,0:T(8,128)(2,1)}, bf16[1,640,2048]{2,1,0:T(8,128)(2,1)}, bf16[1,...) async-done(((bf16[1,640,2048]{2,1,0:T(8,128)(2,1)}, bf16[1,640,2048]{2,1,0:T(8,128)(2,1)}, bf16[1,640,2048]{2,1,0:T(8,128)(2,1)}, ...) | async-done | bytes 15728656 | tf_op jit(solution)/shard_map/psum | solution.py:50
  405.6 6.0 %fusion.24 = f32[]{:T(128)} fusion(bf16[1,2048,640]{2,1,0:T(8,128)(2,1)} %get-tuple-element.13, bf16[1,2048,640]{2,1,0:T(8,128)(2,1)} %get-tuple-element.14), kind=kLoop, calls=%fused_computation.48 | loop fusion | flops 10485759 | bytes 5242884 | tf_op jit(solution)/shard_map/reduce_sum | solution.py:52
  411.5 5.8 %fusion.23 = f32[]{:T(128)} fusion(bf16[1,640,2048]{2,1,0:T(8,128)(2,1)} %get-tuple-element.11, bf16[1,640,2048]{2,1,0:T(8,128)(2,1)} %get-tuple-element.12), kind=kLoop, calls=%fused_computation.47 | loop fusion | flops 10485759 | bytes 5242884 | tf_op jit(solution)/shard_map/reduce_sum | solution.py:52
  417.4 0.0 copy-done.4
  417.4 0.0 copy-done.5
  417.4 3.3 fusion.22
  422.7 0.0 copy-done
  422.7 21.4 %fusion.30 = (bf16[2,2048,640]{2,1,0:T(8,128)(2,1)}, f32[2,2048,640]{2,1,0:T(8,128)}, f32[2,2048,640]{2,1,0:T(8,128)}) fusion(bf16[2,2048,640]{2,1,0:T(8,128)(2,1)} %param.15, f32[]{:T(128)S(6)} %min_shard_map.3, bf16[1,2048,640]{2,1,0:T(8,128)(2,1)S(1)} %copy-done, bf16[1,2048,640]{2,1,0:T(8,128)(2,1)} %get-tuple-element.14, f32[2,2048,640]{2,1,0:T(8,128)} %param.21, ...), kind=kLoop, calls=%fused_computation.54 | loop fusion | flops 52428800 | bytes 57671684 | tf_op jit(solution)/shard_map/convert_element_type | solution.py:30
  444.1 36.1 %fusion.21 = (bf16[2,640,2048]{2,1,0:T(8,128)(2,1)}, f32[2,640,2048]{2,1,0:T(8,128)}, f32[2,640,2048]{2,1,0:T(8,128)}, bf16[2,640,2048]{2,1,0:T(8,128)(2,1)}, f3...) fusion(bf16[2,640,2048]{2,1,0:T(8,128)(2,1)} %param.13, f32[]{:T(128)S(6)} %min_shard_map.3, ...), kind=kLoop, calls=%fused_computation.45 | loop fusion | flops 104857600 | bytes 115343360 | tf_op jit(solution)/shard_map/convert_element_type | solution.py:30
  (11 shorter events, 0.0 us)
Async XLA Ops:
  7.2 398.4 %all-reduce.3.cloned.1.call-start = ((), (), s32[]{:S(2)}) async-start(), calls=%async_computation | async-start | bytes 31457280 | tf_op jit(solution)/shard_map/psum | solution.py:50
  10.3 45.1 %copy-start.2 = (bf16[1,2048,640]{1,2,0:T(8,128)(2,1)}, bf16[1,2048,640]{1,2,0:T(8,128)(2,1)S(1)}, u32[]{:S(2)}) copy-start(bf16[1,2048,640]{1,2,0:T(8,128)(2,1)S(1)} %copy.20) | copy-start | bytes 7864324
  10.8 27.6 %copy-start.11 = (f32[2048]{0:T(1024)}, f32[2048]{0:T(1024)S(1)}, u32[]{:S(2)}) copy-start(f32[2048]{0:T(1024)S(1)} %add_rsqrt_fusion) | copy-start | bytes 24580
  15.6 11.3 %copy-start.8 = (bf16[1,2048,640]{2,1,0:T(8,128)(2,1)S(1)}, bf16[1,2048,640]{2,1,0:T(8,128)(2,1)}, u32[]{:S(2)}) copy-start(bf16[1,2048,640]{2,1,0:T(8,128)(2,1)} %param.11) | copy-start | bytes 7864324
  64.5 1.5 copy-start.6
  64.5 1.5 copy-start.9
  78.2 55.4 %slice-start.2 = ((s8[5242880]{0:T(1024)(128)(4,1)}), s8[1048576]{0:T(1024)(128)(4,1)S(1)}, s32[]{:S(2)}) async-start(s8[5242880]{0:T(1024)(128)(4,1)} %bitcast.76), calls=%async_computation.3 | async-start | bytes 2097152
  103.3 30.2 %slice-start.3 = ((s8[5242880]{0:T(1024)(128)(4,1)}), s8[4194304]{0:T(1024)(128)(4,1)S(1)}, s32[]{:S(2)}) async-start(s8[5242880]{0:T(1024)(128)(4,1)} %bitcast.76), calls=%async_computation.4 | async-start | bytes 8388608
  120.2 36.7 %slice-start = ((s8[5242880]{0:T(1024)(128)(4,1)}), s8[4194304]{0:T(1024)(128)(4,1)S(1)}, s32[]{:S(2)}) async-start(s8[5242880]{0:T(1024)(128)(4,1)} %bitcast.74), calls=%async_computation.1 | async-start | bytes 8388608
  133.5 23.3 %slice-start.1 = ((s8[5242880]{0:T(1024)(128)(4,1)}), s8[1048576]{0:T(1024)(128)(4,1)S(1)}, s32[]{:S(2)}) async-start(s8[5242880]{0:T(1024)(128)(4,1)} %bitcast.74), calls=%async_computation.2 | async-start | bytes 2097152
  145.9 10.9 %copy-start.7 = (bf16[2048,640]{0,1:T(8,128)(2,1)S(1)}, bf16[2048,640]{0,1:T(8,128)(2,1)}, u32[]{:S(2)}) copy-start(bf16[2048,640]{0,1:T(8,128)(2,1)} %copy-done.6) | copy-start | bytes 7864324
  145.9 10.9 %copy-start.14 = (bf16[2048,640]{0,1:T(8,128)(2,1)S(1)}, bf16[2048,640]{0,1:T(8,128)(2,1)}, u32[]{:S(2)}) copy-start(bf16[2048,640]{0,1:T(8,128)(2,1)} %fusion.44) | copy-start | bytes 7864324
  156.9 8.5 %copy-start.10 = (f32[2048]{0:T(1024)S(1)}, f32[2048]{0:T(1024)}, u32[]{:S(2)}) copy-start(f32[2048]{0:T(1024)} %copy-done.9) | copy-start | bytes 24580
  156.9 8.5 %copy-start.1 = (bf16[1,2048,640]{1,2,0:T(8,128)(2,1)S(1)}, bf16[1,2048,640]{1,2,0:T(8,128)(2,1)}, u32[]{:S(2)}) copy-start(bf16[1,2048,640]{1,2,0:T(8,128)(2,1)} %copy.21) | copy-start | bytes 7864324
  165.4 12.5 %slice-start.4 = ((s8[5242880]{0:T(1024)(128)(4,1)}), s8[1048576]{0:T(1024)(128)(4,1)S(1)}, s32[]{:S(2)}) async-start(s8[5242880]{0:T(1024)(128)(4,1)} %bitcast.78), calls=%async_computation.5 | async-start | bytes 2097152
  167.5 10.5 %slice-start.5 = ((s8[5242880]{0:T(1024)(128)(4,1)}), s8[4194304]{0:T(1024)(128)(4,1)S(1)}, s32[]{:S(2)}) async-start(s8[5242880]{0:T(1024)(128)(4,1)} %bitcast.78), calls=%async_computation.6 | async-start | bytes 8388608
  178.0 7.3 %copy-start.3 = (bf16[1,2048,640]{1,2,0:T(8,128)(2,1)S(1)}, bf16[1,2048,640]{1,2,0:T(8,128)(2,1)}, u32[]{:S(2)}) copy-start(bf16[1,2048,640]{1,2,0:T(8,128)(2,1)} %copy-done.2) | copy-start | bytes 7864324
  178.0 7.3 %copy-start.12 = (f32[2048]{0:T(1024)S(1)}, f32[2048]{0:T(1024)}, u32[]{:S(2)}) copy-start(f32[2048]{0:T(1024)} %copy-done.11) | copy-start | bytes 24580
  185.3 13.9 %copy-start.13 = (bf16[2048,2048]{1,0:T(8,128)(2,1)}, bf16[2048,2048]{1,0:T(8,128)(2,1)S(1)}, u32[]{:S(2)}) copy-start(bf16[2048,2048]{1,0:T(8,128)(2,1)S(1)} %convolution_convert_fusion) | copy-start | bytes 25165828
  405.5 11.8 %copy-start.4 = (bf16[1,640,2048]{2,1,0:T(8,128)(2,1)S(1)}, bf16[1,640,2048]{2,1,0:T(8,128)(2,1)}, u32[]{:S(2)}) copy-start(bf16[1,640,2048]{2,1,0:T(8,128)(2,1)} %get-tuple-element.9) | copy-start | bytes 7864324
  405.6 11.8 %copy-start.5 = (bf16[1,640,2048]{2,1,0:T(8,128)(2,1)S(1)}, bf16[1,640,2048]{2,1,0:T(8,128)(2,1)}, u32[]{:S(2)}) copy-start(bf16[1,640,2048]{2,1,0:T(8,128)(2,1)} %get-tuple-element.10) | copy-start | bytes 7864324
  405.6 17.1 %copy-start = (bf16[1,2048,640]{2,1,0:T(8,128)(2,1)S(1)}, bf16[1,2048,640]{2,1,0:T(8,128)(2,1)}, u32[]{:S(2)}) copy-start(bf16[1,2048,640]{2,1,0:T(8,128)(2,1)} %get-tuple-element.13) | copy-start | bytes 7864324
Sparse Core Ops, SparseCore 0:
  218.7 186.8 all-reduce.2
where the time goes:
time: 497 us; the launch traced here: 488 us
  matrix products  199 us (40%)
  waiting for transfers between devices  187 us (38%)
  other arithmetic  75.3 us (15%)
  between operations  16.8 us (3%)
  local copies, waits for them, and re-layouts  9.26 us (2%)
    psum x1, waiting for transfers between devices, step(): summed[number] = [lax.psum(by_w[name], 'dp') for name in NAMES]  187 us
    dot_general x5, matrix products, layer(): gate = jnp.dot(a, w['w_gate'], preferred_element_type=jnp.float32)  75.4 us
    dot_general x5, matrix products, layer(): up = jnp.dot(a, w['w_up'], preferred_element_type=jnp.float32)  68.7 us
    convert_element_type x2, other arithmetic, adamw(): return ((w - 0.02 * step).astype(jnp.bfloat16), m, v)  57.6 us
    dot_general x5, matrix products, matmul(): jnp.dot(a, w, preferred_element_type=jnp.float32).astype(jnp.bfloat16)  55.1 us
    reduce_sum x3, other arithmetic, step(): jnp.sum(g * g)  15.1 us
  transfers between devices with their start and end apart: 1, of which 1 were waited for; matrix products, arithmetic and copies ran while one was open for 0% of the time, Pallas kernels for 0%

commit v1 on v0

v1 whole, which is shorter than its diff:
```python
import functools

import jax
import jax.numpy as jnp
from jax import lax
from jax.experimental import pallas as pl
from jax.experimental.pallas import tpu as pltpu
from jax.sharding import PartitionSpec as P

MESH = pl.DeviceIdType.MESH
F32, BF16 = jnp.float32, jnp.bfloat16
HBM = pl.BlockSpec(memory_space=pltpu.HBM)
BLOCK = 256
LANES = 128
ROWS = 256
VMEM_LIMIT = 66 * 1024 * 1024 - 4 * 1024 * 1024


def sigmoid(x):
    return 0.5 * jnp.tanh(0.5 * x) + 0.5


def dot(a, b, contract=((1,), (0,))):
    return lax.dot_general(a, b, (contract, ((), ())), preferred_element_type=F32)


def scale_of(wide):
    return lax.rsqrt(jnp.mean(wide * wide, -1, keepdims=True) + 1e-6)


def normed(h):
    wide = h.astype(F32)
    return (wide * scale_of(wide)).astype(BF16)


def forward_kernel(x_ref, dy_ref, wg_ref, wu_ref, wd_ref, h_ref, a_ref, at_ref, dyt_ref, act_ref):
    x = x_ref[...]
    a = normed(x)
    a_ref[0] = a
    at_ref[0] = a.T
    dyt_ref[...] = dy_ref[...].T
    width = 2 * BLOCK
    for f in range(0, act_ref.shape[1], width):
        gate = dot(a, wg_ref[0, :, f : f + width])
        up = dot(a, wu_ref[0, :, f : f + width])
        act_ref[:, f : f + width] = (gate * sigmoid(gate) * up).astype(BF16)
    h = x + dot(act_ref[...], wd_ref[0]).astype(BF16)
    h_ref[...] = h
    b = normed(h)
    a_ref[1] = b
    at_ref[1] = b.T


def forward(x, dy, wg, wu, wd):
    tokens, d = x.shape
    ff = wg.shape[2]
    rows = min(512, tokens)
    tile = pl.BlockSpec((rows, d), lambda i: (i, 0))
    return pl.pallas_call(
        forward_kernel,
        grid=(tokens // rows,),
        in_specs=[tile, tile]
        + [pl.BlockSpec((1, d, ff), lambda i: (0, 0, 0))] * 2
        + [pl.BlockSpec((1, ff, d), lambda i: (0, 0, 0))],
        out_specs=[
            tile,
            pl.BlockSpec((2, rows, d), lambda i: (0, i, 0)),
            pl.BlockSpec((2, d, rows), lambda i: (0, 0, i)),
            pl.BlockSpec((d, rows), lambda i: (0, i)),
        ],
        out_shape=[
            jax.ShapeDtypeStruct((tokens, d), BF16),
            jax.ShapeDtypeStruct((2, tokens, d), BF16),
            jax.ShapeDtypeStruct((2, d, tokens), BF16),
            jax.ShapeDtypeStruct((d, tokens), BF16),
        ],
        scratch_shapes=[pltpu.VMEM((rows, ff), BF16)],
        compiler_params=pltpu.CompilerParams(vmem_limit_bytes=VMEM_LIMIT),
    )(x, dy, wg, wu, wd)


def backward_kernel(
    chips, a_hbm, at_hbm, dy_hbm, dyt_hbm, h_hbm, wg_hbm, wu_hbm, wd_hbm, sums,
    a_ref, at_ref, dy_ref, dyt_ref, h_ref, wg_ref, wu_ref, wd_ref, p_ref, dg_ref, du_ref, dag_ref, dau_ref,
    own_ref, got_ref, both_ref, land_ref,
    load_sem, w_sem, pair_send, pair_recv, rs_send, rs_recv, ag_send, ag_recv, share_send, share_recv, keep_sem,
):
    layers, tokens, d = a_ref.shape
    ff = wg_hbm.shape[2]
    per_layer = ff // BLOCK
    blocks = layers * per_layer
    chunk = 3 * d // chips
    tiles = tokens // ROWS
    first_tiles = tiles * 3 // 4

    me = lax.axis_index("dp")
    z, core = me // 2, me % 2
    other = 1 - core
    partner = {"dp": z * 2 + other}

    def along(step):
        return {"dp": lax.rem(z + step + chips, chips) * 2 + core}

    def rows_of(c):
        return pl.ds(pl.multiple_of(c * chunk, chunk), chunk)

    def weights(t, slot):
        layer = layers - 1 - t // per_layer
        f = pl.multiple_of(lax.rem(t, per_layer) * BLOCK, BLOCK)
        return [
            pltpu.make_async_copy(wg_hbm.at[layer, :, pl.ds(f, BLOCK)], wg_ref.at[slot], w_sem.at[slot, 0]),
            pltpu.make_async_copy(wu_hbm.at[layer, :, pl.ds(f, BLOCK)], wu_ref.at[slot], w_sem.at[slot, 1]),
            pltpu.make_async_copy(wd_hbm.at[layer, pl.ds(f, BLOCK), :], wd_ref.at[slot], w_sem.at[slot, 2]),
        ]

    last = layers - 1
    loads = [
        pltpu.make_async_copy(a_hbm.at[last], a_ref.at[last], load_sem.at[0]),
        pltpu.make_async_copy(dy_hbm, dy_ref, load_sem.at[1]),
        pltpu.make_async_copy(at_hbm.at[last], at_ref.at[last], load_sem.at[2]),
        pltpu.make_async_copy(dyt_hbm, dyt_ref, load_sem.at[3]),
        pltpu.make_async_copy(h_hbm, h_ref, load_sem.at[4]),
        pltpu.make_async_copy(a_hbm.at[0], a_ref.at[0], load_sem.at[5]),
        pltpu.make_async_copy(at_hbm.at[0], at_ref.at[0], load_sem.at[6]),
    ]
    loads[0].start()
    for copy in weights(0, 0):
        copy.start()
    for copy in loads[1:]:
        copy.start()

    barrier = pltpu.get_barrier_semaphore()
    for peer in (partner, along(1), along(-1)):
        pl.semaphore_signal(barrier, inc=1, device_id=peer, device_id_type=MESH)
    pl.semaphore_wait(barrier, 3)

    def pair_copy(b):
        slot = lax.rem(b, 2)
        return pltpu.make_async_remote_copy(
            own_ref.at[slot, other], got_ref.at[slot], pair_send.at[slot], pair_recv.at[slot], partner, MESH
        )

    def rs_copy(b, s):
        way = 1 - 2 * lax.rem(b, 2)
        return pltpu.make_async_remote_copy(
            land_ref.at[b, s - 1], land_ref.at[b, s], rs_send.at[b, s - 1], rs_recv.at[b, s - 1], along(way), MESH
        )

    def ag_copy(src, b, c, side, hop):
        way = (1 - 2 * lax.rem(b, 2)) * (1 - 2 * side)
        place = side * (chips // 2) + hop - 1
        return pltpu.make_async_remote_copy(
            src, sums.at[b, core, rows_of(c), :], ag_send.at[b, place], ag_recv.at[b, place], along(way), MESH
        )

    def share_copy(src, b, c):
        return pltpu.make_async_remote_copy(src, sums.at[b, core, rows_of(c), :], share_send, share_recv, partner, MESH)

    def keep_copy(b):
        return pltpu.make_async_copy(land_ref.at[b, chips - 1], sums.at[b, core, rows_of(z), :], keep_sem.at[b])

    hops = (chips // 2, chips - 1 - chips // 2)

    def tick(u, odd):
        if not odd:
            b = u - 1

            @pl.when((b >= 0) & (b < blocks))
            def _():
                slot = lax.rem(b, 2)
                pair_copy(b).wait()

                def add(i, _):
                    r = pl.ds(pl.multiple_of(i * chunk, chunk), chunk)
                    both_ref[lax.rem(b, 4), r] = own_ref[slot, core, r].astype(F32) + got_ref[slot, r].astype(F32)
                    return 0

                lax.fori_loop(0, chips, add, 0)

        steps = [s for s in range(chips, 0, -1) if (s + odd) % 2 == 1]
        for s in steps:
            b = u - (s + 1) // 2 if not odd else u - s // 2

            @pl.when((b >= 0) & (b < blocks))
            def _(s=s, b=b):
                way = 1 - 2 * lax.rem(b, 2)
                term = both_ref[lax.rem(b, 4), rows_of(lax.rem(z - way * s + 2 * chips, chips))]
                if s > 1:
                    rs_copy(b, s - 1).wait_recv()
                    term = term + land_ref[b, s - 1].astype(F32)
                land_ref[b, s - 1] = term.astype(BF16)

        for s in steps:
            b = u - (s + 1) // 2 if not odd else u - s // 2

            @pl.when((b >= 0) & (b < blocks))
            def _(s=s, b=b):
                if s < chips:
                    rs_copy(b, s).start()
                else:
                    src = land_ref.at[b, chips - 1]
                    for side in range(2):
                        ag_copy(src, b, z, side, 1).start()
                    share_copy(src, b, z).start()
                    keep_copy(b).start()

        for hop in range(1, hops[0] + 1):
            if (chips + 1 + hop + odd) % 2:
                continue
            b = u - (chips + 1 + hop - odd) // 2

            @pl.when((b >= 0) & (b < blocks))
            def _(hop=hop, b=b):
                for side in range(2):
                    if hop > hops[side]:
                        continue
                    way = (1 - 2 * lax.rem(b, 2)) * (1 - 2 * side)
                    c = lax.rem(z - way * hop + 2 * chips, chips)
                    ag_copy(sums.at[b, core, rows_of(c), :], b, c, side, hop).wait_recv()
                    if hop < hops[side]:
                        ag_copy(sums.at[b, core, rows_of(c), :], b, c, side, hop + 1).start()
                    share_copy(sums.at[b, core, rows_of(c), :], b, c).start()

    def token_tile(t, layer, slot, i):
        r = pl.ds(pl.multiple_of(i * ROWS, ROWS), ROWS)
        a = a_ref[layer, r]
        wg, wu = wg_ref[slot], wu_ref[slot]
        gate, up = dot(a, wg), dot(a, wu)
        by_p = dot(dy_ref[r], wd_ref[slot], ((1,), (1,))).astype(BF16).astype(F32)
        s = sigmoid(gate)
        silu = gate * s
        p_ref[r] = (silu * up).astype(BF16)
        by_up = (by_p * silu).astype(BF16)
        by_gate = (by_p * up * (s + silu * (1.0 - s))).astype(BF16)
        dg_ref[r] = by_gate
        du_ref[r] = by_up

        @pl.when(layer > 0)
        def _():
            by_g, by_u = dot(by_gate, wg, ((1,), (1,))), dot(by_up, wu, ((1,), (1,)))
            start = lax.rem(t, per_layer) == 0

            @pl.when(start)
            def _():
                dag_ref[r] = by_g
                dau_ref[r] = by_u

            @pl.when(jnp.logical_not(start))
            def _():
                dag_ref[r] += by_g
                dau_ref[r] += by_u

    def next_layer(i, _):
        r = pl.ds(pl.multiple_of(i * ROWS, ROWS), ROWS)
        wide = h_ref[r].astype(F32)
        by_a = (dag_ref[r].astype(BF16).astype(F32) + dau_ref[r].astype(BF16).astype(F32)).astype(BF16).astype(F32)
        scale = scale_of(wide)
        inner = jnp.sum(by_a * wide, -1, keepdims=True) * (scale * scale * scale / d)
        by_h = dy_ref[r] + (by_a * scale - wide * inner).astype(BF16)
        dy_ref[r] = by_h
        dyt_ref[:, r] = by_h.T
        return 0

    def block(t, _):
        slot = lax.rem(t, 2)
        layer = layers - 1 - t // per_layer

        @pl.when(t + 1 < blocks)
        def _():
            for copy in weights(t + 1, 1 - slot):
                copy.start()

        @pl.when(t == 0)
        def _():
            loads[0].wait()
            loads[1].wait()

        @pl.when(t == per_layer)
        def _():
            for copy in loads[4:]:
                copy.wait()
            lax.fori_loop(0, tiles, next_layer, 0)

        for copy in weights(t, slot):
            copy.wait()

        def some(i, _):
            token_tile(t, layer, slot, i)
            return 0

        lax.fori_loop(0, first_tiles, some, 0)
        tick(t, 0)
        lax.fori_loop(first_tiles, tiles, some, 0)

        @pl.when(t == 0)
        def _():
            loads[2].wait()
            loads[3].wait()

        for place, (left, right) in enumerate(
            ((at_ref.at[layer], dg_ref), (at_ref.at[layer], du_ref), (dyt_ref, p_ref))
        ):
            g = dot(left[...], right[...]).astype(BF16)
            for half in range(2):
                own_ref[slot, half, place * d : (place + 1) * d, :] = g[:, half * LANES : (half + 1) * LANES]
        tick(t, 1)
        pair_copy(t).start()
        return 0

    lax.fori_loop(0, blocks, block, 0)

    def drain(u, _):
        tick(u, 0)
        tick(u, 1)
        return 0

    lax.fori_loop(blocks, (2 * (blocks - 1) + chips + 1 + hops[0]) // 2 + 1, drain, 0)

    def finish(b, _):
        for s in range(1, chips):
            rs_copy(b, s).wait_send()
        for side in range(2):
            for hop in range(1, hops[side] + 1):
                ag_copy(land_ref.at[b, chips - 1], b, z, side, hop).wait_send()
        keep_copy(b).wait()
        return 0

    lax.fori_loop(0, blocks, finish, 0)
    pltpu.make_async_copy(sums.at[:, core], sums.at[:, core], share_send).wait()
    pltpu.make_async_copy(sums.at[:, other], sums.at[:, other], share_recv).wait()


def backward(chips, a, at, dy, dyt, h, wg, wu, wd):
    layers, tokens, d = a.shape
    ff = wg.shape[2]
    blocks = layers * ff // BLOCK
    chunk = 3 * d // chips
    vmem = pltpu.VMEM
    sem = pltpu.SemaphoreType.DMA
    flops = 2 * tokens * d * ff * (6 * layers + 2)
    return pl.pallas_call(
        functools.partial(backward_kernel, chips),
        out_shape=jax.ShapeDtypeStruct((blocks, 2, 3 * d, LANES), BF16),
        in_specs=[HBM] * 8,
        out_specs=HBM,
        scratch_shapes=[
            vmem((layers, tokens, d), BF16), vmem((layers, d, tokens), BF16), vmem((tokens, d), BF16), vmem((d, tokens), BF16),
            vmem((tokens, d), BF16), vmem((2, d, BLOCK), BF16), vmem((2, d, BLOCK), BF16), vmem((2, BLOCK, d), BF16),
            vmem((tokens, BLOCK), BF16), vmem((tokens, BLOCK), BF16), vmem((tokens, BLOCK), BF16),
            vmem((tokens, d), F32), vmem((tokens, d), F32),
            vmem((2, 2, 3 * d, LANES), BF16), vmem((2, 3 * d, LANES), BF16), vmem((4, 3 * d, LANES), F32),
            vmem((blocks, chips, chunk, LANES), BF16),
            sem((7,)), sem((2, 3)), sem((2,)), sem((2,)), sem((blocks, chips - 1)), sem((blocks, chips - 1)),
            sem((blocks, chips - 1)), sem((blocks, chips - 1)), sem, sem, sem((blocks,)),
        ],
        compiler_params=pltpu.CompilerParams(collective_id=0, has_side_effects=True, vmem_limit_bytes=VMEM_LIMIT),
        cost_estimate=pl.CostEstimate(flops=flops, bytes_accessed=64 << 20, transcendentals=0),
    )(a, at, dy, dyt, h, wg, wu, wd)


def adamw_kernel(count, sums, *refs):
    ins, outs, (g_ref, factor_ref, sem) = refs[:9], refs[9:18], refs[18:]
    blocks, _, d3, _ = sums.shape
    d = d3 // 3
    b = pl.program_id(0)

    @pl.when(b == 0)
    def _():
        def load(i):
            return pltpu.make_async_copy(sums.at[i], g_ref.at[i], sem.at[i])

        def start(i, _):
            load(i).start()
            return 0

        def square(i, total):
            load(i).wait()

            def some(k, total):
                r = pl.ds(pl.multiple_of(k * LANES, LANES), LANES)
                for half in range(2):
                    g = g_ref[i, half, r].astype(F32).reshape(LANES // 8, 8, LANES)
                    total = total + jnp.sum(g * g, axis=0)
                return total

            return lax.fori_loop(0, d3 // LANES, some, total)

        lax.fori_loop(0, blocks, start, 0)
        total = lax.fori_loop(0, blocks, square, jnp.zeros((8, LANES), F32))
        total = jnp.sum(jnp.sum(total, axis=1, keepdims=True), axis=0, keepdims=True)
        factor = jnp.minimum(1.0, 0.5 * lax.rsqrt(total / count + 1e-30))
        factor_ref[...] = jnp.broadcast_to(factor, factor_ref.shape)

    factor = factor_ref[0:1, :]
    for place in range(3):
        w_ref, m_ref, v_ref = (ins[3 * kind + place] for kind in range(3))
        w_out, m_out, v_out = (outs[3 * kind + place] for kind in range(3))
        for half in range(2):
            for k in range(0, d, LANES):
                g = g_ref[b, half, place * d + k : place * d + k + LANES, :].astype(F32)
                if place < 2:
                    at = (0, slice(k, k + LANES), slice(half * LANES, (half + 1) * LANES))
                else:
                    g = g.T
                    at = (0, slice(half * LANES, (half + 1) * LANES), slice(k, k + LANES))
                g = g * factor
                m = 0.9 * m_ref[at] + 0.1 * g
                v = 0.95 * v_ref[at] + 0.05 * g * g
                w = w_ref[at].astype(F32)
                w_out[at] = (w - 0.02 * (m * lax.rsqrt(v + 1e-8) + 0.1 * w)).astype(BF16)
                m_out[at] = m
                v_out[at] = v


def adamw(sums, arrays):
    layers, d, ff = arrays[0].shape
    per_layer = ff // BLOCK
    blocks = layers * per_layer
    wide = pl.BlockSpec((1, d, BLOCK), lambda b: (layers - 1 - b // per_layer, 0, b % per_layer))
    tall = pl.BlockSpec((1, BLOCK, d), lambda b: (layers - 1 - b // per_layer, b % per_layer, 0))
    specs = [wide, wide, tall] * 3
    return pl.pallas_call(
        functools.partial(adamw_kernel, 3 * layers * d * ff),
        grid=(blocks,),
        in_specs=[HBM] + specs,
        out_specs=specs,
        out_shape=[jax.ShapeDtypeStruct(a.shape, a.dtype) for a in arrays],
        scratch_shapes=[
            pltpu.VMEM((blocks, 2, 3 * d, LANES), BF16),
            pltpu.VMEM((8, LANES), F32),
            pltpu.SemaphoreType.DMA((blocks,)),
        ],
        compiler_params=pltpu.CompilerParams(vmem_limit_bytes=VMEM_LIMIT),
    )(sums, *arrays)


def solution(mesh):
    chips = mesh.shape["dp"] // 2

    def step(x, dy, *arrays):
        x, dy = x[0], dy[0]
        wg, wu, wd = arrays[:3]
        h, a, at, dyt = forward(x, dy, wg, wu, wd)
        sums = backward(chips, a, at, dy, dyt, h, wg, wu, wd)
        return tuple(adamw(sums, arrays))

    return jax.shard_map(
        step,
        mesh=mesh,
        in_specs=(P(("rep", "dp"), None, None),) * 2 + (P(None, None, None),) * 9,
        out_specs=(P("rep", None, None),) * 9,
        check_vma=False,
    )
```

time: 497 us -> 342 us (0.69); the launches traced: 488 us -> 342 us
  Pallas kernels: 0 us -> 341 us
  matrix products: 199 us -> 0 us
  waiting for transfers between devices: 187 us -> 0 us
  other arithmetic: 75.3 us -> 0 us
  between operations: 16.8 us -> 0.65 us
  local copies, waits for them, and re-layouts: 9.26 us -> 0 us
    pallas_call x0 -> x3, Pallas kernels: none -> 341 us  [the longest x1 255 us: backward(): pl.pallas_call(functools.partial(backward_kernel, chips), out_shape=jax.S...]
    dot_general x15 -> x0, matrix products: 199 us -> none  [the longest x5 75.4 us: layer(): gate = jnp.dot(a, w['w_gate'], preferred_element_type=jnp.float32)]
    psum x1 -> x0, waiting for transfers between devices: 187 us -> none  [step(): summed[number] = [lax.psum(by_w[name], 'dp') for name in NAMES]]
    convert_element_type x2 -> x0, other arithmetic: 57.6 us -> none  [adamw(): return ((w - 0.02 * step).astype(jnp.bfloat16), m, v)]
    reduce_sum x4 -> x0, other arithmetic: 15.7 us -> none  [the longest x3 15.1 us: step(): jnp.sum(g * g)]
    unnamed x44 -> x0, local copies, waits for them, and re-layouts: 9.26 us -> none
  transfers between devices with their start and end apart: 1 -> 0, of which waited for: 1 -> 0; matrix products, arithmetic and copies ran while one was open for 0% -> 0% of each run, Pallas kernels for 0% -> 0%
where the time goes in v1:
time: 342 us
  Pallas kernels  341 us (100%)
    pallas_call x1, Pallas kernels, backward(): pl.pallas_call(functools.partial(backward_kernel, chips), out_shape=jax.S...  255 us
    pallas_call x1, Pallas kernels, adamw(): pl.pallas_call(functools.partial(adamw_kernel, 3 * layers * d * ff), grid...  59.2 us
    pallas_call x1, Pallas kernels, forward(): pl.pallas_call(forward_kernel, grid=(tokens // rows,), in_specs=[tile, ti...  27.5 us

profile of v1, /device:TPU:21, one launch (start us, length us, event | category | flops | bytes accessed | tf_op | source)
XLA Modules:
  0.0 342.1 jit_solution(9844913563675128808)
XLA Ops:
  0.6 27.5 %shard_map.178 = (bf16[2048,640]{1,0:T(8,128)(2,1)}, bf16[2,2048,640]{2,1,0:T(8,128)(2,1)}, bf16[2,640,2048]{2,1,0:T(8,128)(2,1)}, bf16[640,2048]{1,0:T(8,128)(2,1)}) custom-call(bf16[2048,640]{1,0:T(8,128)(2,1)} %bitcast.2, bf16[2048,640]{1,0:T(8,128)(2,1)} %bitcast.3, bf16[2,640,2048]{2,1,0:T(8,128)(2,1)} %refs_0_.1, bf16[2,640,2048]{2,1,0:T(8,128)(2,1)} %refs_1_.1, ...), custom_call_target="tpu_custom_call" | custom-call | tf_op jit(solution)/shard_map/pallas_call | solution.py:59
  28.2 254.8 %shard_map.179.sums = bf16[16,2,1920,128]{3,2,1,0:T(8,128)(2,1)} custom-call(bf16[2,2048,640]{2,1,0:T(8,128)(2,1)} %get-tuple-element.13.a_hbm, bf16[2,640,2048]{2,1,0:T(8,128)(2,1)} %get-tuple-element.14.at_hbm, bf16[2048,640]{1,0:T(8,128)(2,1)} %bitcast.4, bf16[640,2048]{1,0:T(8,128)(2,1)} %get-tuple-element.15.dyt_hbm, ...), custom_call_target="tpu_custom_call" | custom-call | flops 75161927680 | bytes 67108864 | tf_op jit(solution)/shard_map/pallas_call | solution.py:341
  283.0 59.2 %shard_map.180 = (bf16[2,640,2048]{2,1,0:T(8,128)(2,1)}, bf16[2,640,2048]{2,1,0:T(8,128)(2,1)}, bf16[2,2048,640]{2,1,0:T(8,128)(2,1)}, f32[2,640,2048]{2,1,0:T(8...) custom-call(bf16[16,2,1920,128]{3,2,1,0:T(8,128)(2,1)} %shard_map.17, ...), custom_call_target="tpu_custom_call" | custom-call | tf_op jit(solution)/shard_map/pallas_call | solution.py:422

commit v2 on v1

v2 whole, which is shorter than its diff:
```python
import functools

import jax
import jax.numpy as jnp
from jax import lax
from jax.experimental import pallas as pl
from jax.experimental.pallas import tpu as pltpu
from jax.sharding import PartitionSpec as P

MESH = pl.DeviceIdType.MESH
F32, BF16 = jnp.float32, jnp.bfloat16
HBM = pl.BlockSpec(memory_space=pltpu.HBM)
BLOCK = 256
LANES = 128
ROWS = 256
VMEM_LIMIT = 67_000_000


def sigmoid(x):
    return 0.5 * jnp.tanh(0.5 * x) + 0.5


def dot(a, b, contract=((1,), (0,))):
    return lax.dot_general(a, b, (contract, ((), ())), preferred_element_type=F32)


def scale_of(wide):
    return lax.rsqrt(jnp.mean(wide * wide, -1, keepdims=True) + 1e-6)


def normed(h):
    wide = h.astype(F32)
    return (wide * scale_of(wide)).astype(BF16)


def forward_kernel(x_ref, dy_ref, wg_ref, wu_ref, wd_ref, h_ref, a_ref, at_ref, dyt_ref, act_ref):
    x = x_ref[...]
    a = normed(x)
    a_ref[0] = a
    at_ref[0] = a.T
    dyt_ref[...] = dy_ref[...].T
    width = 2 * BLOCK
    for f in range(0, act_ref.shape[1], width):
        gate = dot(a, wg_ref[0, :, f : f + width])
        up = dot(a, wu_ref[0, :, f : f + width])
        act_ref[:, f : f + width] = (gate * sigmoid(gate) * up).astype(BF16)
    h = x + dot(act_ref[...], wd_ref[0]).astype(BF16)
    h_ref[...] = h
    b = normed(h)
    a_ref[1] = b
    at_ref[1] = b.T


def forward(x, dy, wg, wu, wd):
    tokens, d = x.shape
    ff = wg.shape[2]
    rows = min(512, tokens)
    tile = pl.BlockSpec((rows, d), lambda i: (i, 0))
    return pl.pallas_call(
        forward_kernel,
        grid=(tokens // rows,),
        in_specs=[tile, tile]
        + [pl.BlockSpec((1, d, ff), lambda i: (0, 0, 0))] * 2
        + [pl.BlockSpec((1, ff, d), lambda i: (0, 0, 0))],
        out_specs=[
            tile,
            pl.BlockSpec((2, rows, d), lambda i: (0, i, 0)),
            pl.BlockSpec((2, d, rows), lambda i: (0, 0, i)),
            pl.BlockSpec((d, rows), lambda i: (0, i)),
        ],
        out_shape=[
            jax.ShapeDtypeStruct((tokens, d), BF16),
            jax.ShapeDtypeStruct((2, tokens, d), BF16),
            jax.ShapeDtypeStruct((2, d, tokens), BF16),
            jax.ShapeDtypeStruct((d, tokens), BF16),
        ],
        scratch_shapes=[pltpu.VMEM((rows, ff), BF16)],
        compiler_params=pltpu.CompilerParams(vmem_limit_bytes=VMEM_LIMIT),
    )(x, dy, wg, wu, wd)


TICKS = 5
LAG = 4
DEPTH = 4


def backward_kernel(
    chips, a_hbm, at_hbm, dy_hbm, dyt_hbm, h_hbm, wg_hbm, wu_hbm, wd_hbm, sums,
    a_ref, at_ref, dy_ref, dyt_ref, h_ref, wg_ref, wu_ref, wd_ref, allg_ref, allu_ref, p_ref, dg_ref, du_ref,
    own_ref, got_ref, both_ref, land_ref,
    load_sem, w_sem, pair_send, pair_recv, rs_send, rs_recv, ag_send, ag_recv, share_send, share_recv, keep_sem,
):
    layers, tokens, d = a_hbm.shape
    ff = wg_hbm.shape[2]
    per_layer = ff // BLOCK
    blocks = layers * per_layer
    slots = blocks + layers - 1
    chunk = 3 * d // chips
    tiles = tokens // ROWS
    near = chips // 2
    far = chips - 1 - near
    inverse = next(i for i in range(TICKS) if i * LAG % TICKS == 1)

    me = lax.axis_index("dp")
    z, core = me // 2, me % 2
    other = 1 - core
    partner = {"dp": z * 2 + other}

    def wrap(c):
        return lax.rem(c + 2 * chips, chips)

    def along(step):
        return {"dp": wrap(z + step) * 2 + core}

    def rows_of(c):
        return pl.ds(pl.multiple_of(c * chunk, chunk), chunk)

    def block_of(t):
        return t - t // (per_layer + 1)

    def is_block(t):
        return (t >= 0) & (t < slots) & (lax.rem(t, per_layer + 1) != per_layer)

    def weights(b, slot):
        layer = layers - 1 - b // per_layer
        f = pl.multiple_of(lax.rem(b, per_layer) * BLOCK, BLOCK)
        return [
            pltpu.make_async_copy(wg_hbm.at[layer, :, pl.ds(f, BLOCK)], wg_ref.at[slot], w_sem.at[slot, 0]),
            pltpu.make_async_copy(wu_hbm.at[layer, :, pl.ds(f, BLOCK)], wu_ref.at[slot], w_sem.at[slot, 1]),
            pltpu.make_async_copy(wd_hbm.at[layer, pl.ds(f, BLOCK), :], wd_ref.at[slot], w_sem.at[slot, 2]),
        ]

    last = layers - 1
    loads = [
        pltpu.make_async_copy(a_hbm.at[last], a_ref, load_sem.at[0]),
        pltpu.make_async_copy(dy_hbm, dy_ref, load_sem.at[1]),
        pltpu.make_async_copy(at_hbm.at[last], at_ref, load_sem.at[2]),
        pltpu.make_async_copy(dyt_hbm, dyt_ref, load_sem.at[3]),
        pltpu.make_async_copy(wg_hbm.at[last], allg_ref, load_sem.at[4]),
        pltpu.make_async_copy(wu_hbm.at[last], allu_ref, load_sem.at[5]),
        pltpu.make_async_copy(h_hbm, h_ref, load_sem.at[6]),
        pltpu.make_async_copy(a_hbm.at[0], a_ref, load_sem.at[7]),
        pltpu.make_async_copy(at_hbm.at[0], at_ref, load_sem.at[8]),
    ]
    loads[0].start()
    for copy in weights(0, 0):
        copy.start()
    for copy in loads[1:7]:
        copy.start()

    barrier = pltpu.get_barrier_semaphore()
    for peer in (partner, along(1), along(-1)):
        pl.semaphore_signal(barrier, inc=1, device_id=peer, device_id_type=MESH)
    pl.semaphore_wait(barrier, 3)

    def pair_copy(b):
        slot = lax.rem(b, 2)
        return pltpu.make_async_remote_copy(
            own_ref.at[slot, other], got_ref.at[slot], pair_send.at[slot], pair_recv.at[slot], partner, MESH
        )

    def way_of(b, side):
        return (1 - 2 * lax.rem(b, 2)) * (1 - 2 * side)

    def rs_place(side, s):
        return side * (near + 1) + s

    def rs_copy(b, side, s):
        sem = side * near + s - 1
        return pltpu.make_async_remote_copy(
            land_ref.at[b, rs_place(side, s - 1)], land_ref.at[b, rs_place(side, s)],
            rs_send.at[b, sem], rs_recv.at[b, sem], along(way_of(b, side)), MESH,
        )

    def ag_copy(src, b, c, side, hop):
        sem = side * near + hop - 1
        return pltpu.make_async_remote_copy(
            src, sums.at[b, core, rows_of(c), :], ag_send.at[b, sem], ag_recv.at[b, sem], along(way_of(b, side)), MESH
        )

    def share_copy(src, b, c):
        return pltpu.make_async_remote_copy(src, sums.at[b, core, rows_of(c), :], share_send, share_recv, partner, MESH)

    def done(b):
        return land_ref.at[b, rs_place(0, near)]

    def keep_copy(b):
        return pltpu.make_async_copy(done(b), sums.at[b, core, rows_of(z), :], keep_sem.at[b])

    def scatter_step(b, s):
        four = lax.rem(b, DEPTH)

        @pl.when(s == 1)
        def _():
            slot = lax.rem(b, 2)
            pair_copy(b).wait()

            def add(i, _):
                r = rows_of(i)
                both_ref[four, r] = own_ref[slot, core, r].astype(F32) + got_ref[slot, r].astype(F32)
                return 0

            lax.fori_loop(0, chips, add, 0)
            for side, reach in ((0, near), (1, far)):
                c = wrap(z + way_of(b, side) * reach)
                land_ref[b, rs_place(side, 0)] = both_ref[four, rows_of(c)].astype(BF16)

        for side, reach in ((0, near), (1, far)):

            @pl.when((s > 1) & (s <= reach))
            def _(side=side, reach=reach):
                rs_copy(b, side, s - 1).wait_recv()
                here = rs_place(side, s - 1)
                c = wrap(z + way_of(b, side) * (reach + 1 - s))
                land_ref[b, here] = (land_ref[b, here].astype(F32) + both_ref[four, rows_of(c)]).astype(BF16)

        @pl.when(s == near + 1)
        def _():
            rs_copy(b, 0, near).wait_recv()
            rs_copy(b, 1, far).wait_recv()
            total = both_ref[four, rows_of(z)] + land_ref[b, rs_place(1, far)].astype(F32)
            land_ref[b, rs_place(0, near)] = (total + land_ref[b, rs_place(0, near)].astype(F32)).astype(BF16)

        for side, reach in ((0, near), (1, far)):

            @pl.when(s <= reach)
            def _(side=side):
                rs_copy(b, side, s).start()

        @pl.when(s == near + 1)
        def _():
            for side in range(2):
                ag_copy(done(b), b, z, side, 1).start()
            share_copy(done(b), b, z).start()
            keep_copy(b).start()

    def gather_step(b, hop):
        for side, reach in ((0, near), (1, far)):

            @pl.when(hop <= reach)
            def _(side=side, reach=reach):
                c = wrap(z - way_of(b, side) * hop)
                here = sums.at[b, core, rows_of(c), :]
                ag_copy(here, b, c, side, hop).wait_recv()

                @pl.when(hop < reach)
                def _():
                    ag_copy(here, b, c, side, hop + 1).start()

                share_copy(here, b, c).start()

    def tick(now):
        first = lax.rem(inverse * now, TICKS)
        for p, step in ((first, scatter_step), (first + TICKS, gather_step)):
            t = (now - LAG * p + 16 * TICKS) // TICKS - 17
            ok = is_block(t)
            if step is gather_step:
                ok = ok & (p < near + 1 + near)

            @pl.when(ok)
            def _(t=t, step=step):
                step(block_of(t), first + 1)

    def token_tiles(slot, kept, first, count):
        for i in range(count):
            r = pl.ds(pl.multiple_of((first + i) * ROWS, ROWS), ROWS)
            a = a_ref[r]
            gate, up = dot(a, wg_ref[slot]), dot(a, wu_ref[slot])
            by_p = dot(dy_ref[r], wd_ref[slot], ((1,), (1,))).astype(BF16).astype(F32)
            s = sigmoid(gate)
            silu = gate * s
            p_ref[r] = (silu * up).astype(BF16)
            du_ref[kept, r] = (by_p * silu).astype(BF16)
            dg_ref[kept, r] = (by_p * up * (s + silu * (1.0 - s))).astype(BF16)

    def next_layer(first, count):
        for i in range(count):
            r = pl.ds(pl.multiple_of((first + i) * ROWS, ROWS), ROWS)
            wide = h_ref[r].astype(F32)

            def through(by_ref, w_ref):
                total = jnp.zeros((ROWS, d), F32)
                for k in range(per_layer):
                    total = total + dot(by_ref[k, r], w_ref[:, k * BLOCK : (k + 1) * BLOCK], ((1,), (1,)))
                return total.astype(BF16).astype(F32)

            by_a = (through(dg_ref, allg_ref) + through(du_ref, allu_ref)).astype(BF16).astype(F32)
            scale = scale_of(wide)
            inner = jnp.sum(by_a * wide, -1, keepdims=True) * (scale * scale * scale / d)
            by_h = dy_ref[r] + (by_a * scale - wide * inner).astype(BF16)
            dy_ref[r] = by_h
            dyt_ref[:, r] = by_h.T

    parts = TICKS - 1
    each = tiles // parts

    def slot_of_work(t, _):
        @pl.when(is_block(t))
        def _():
            b = block_of(t)
            slot = lax.rem(b, 2)
            kept = lax.rem(b, per_layer)

            @pl.when(b + 1 < blocks)
            def _():
                for copy in weights(b + 1, 1 - slot):
                    copy.start()

            @pl.when(t == 0)
            def _():
                loads[0].wait()
                loads[1].wait()

            for copy in weights(b, slot):
                copy.wait()

            def part(i, _):
                token_tiles(slot, kept, i * each, each)
                tick(TICKS * t + i)
                return 0

            lax.fori_loop(0, parts, part, 0)

            @pl.when(t == 0)
            def _():
                loads[2].wait()
                loads[3].wait()

            for place, (left, right) in enumerate(
                ((at_ref, dg_ref.at[kept]), (at_ref, du_ref.at[kept]), (dyt_ref, p_ref))
            ):
                g = dot(left[...], right[...]).astype(BF16)
                for half in range(2):
                    own_ref[slot, half, place * d : (place + 1) * d, :] = g[:, half * LANES : (half + 1) * LANES]
            pair_copy(b).start()
            tick(TICKS * t + parts)

        @pl.when(jnp.logical_not(is_block(t)))
        def _():
            for copy in loads[7:]:
                copy.start()
            for copy in loads[4:7]:
                copy.wait()

            def part(i, _):
                next_layer(i * each, each)
                tick(TICKS * t + i)
                return 0

            lax.fori_loop(0, parts, part, 0)
            tick(TICKS * t + parts)
            for copy in loads[7:]:
                copy.wait()

        return 0

    lax.fori_loop(0, slots, slot_of_work, 0)

    def drain(now, _):
        tick(now)
        return 0

    lax.fori_loop(TICKS * slots, TICKS * slots + LAG * 2 * near + 1, drain, 0)

    def finish(b, _):
        for side, reach in ((0, near), (1, far)):
            for hop in range(1, reach + 1):
                rs_copy(b, side, hop).wait_send()
                ag_copy(done(b), b, z, side, hop).wait_send()
        keep_copy(b).wait()
        return 0

    lax.fori_loop(0, blocks, finish, 0)
    pltpu.make_async_copy(sums.at[:, core], sums.at[:, core], share_send).wait()
    pltpu.make_async_copy(sums.at[:, other], sums.at[:, other], share_recv).wait()


def backward(chips, a, at, dy, dyt, h, wg, wu, wd):
    layers, tokens, d = a.shape
    ff = wg.shape[2]
    per_layer = ff // BLOCK
    blocks = layers * per_layer
    chunk = 3 * d // chips
    vmem = pltpu.VMEM
    sem = pltpu.SemaphoreType.DMA
    flops = 2 * tokens * d * ff * (6 * layers + 2)
    return pl.pallas_call(
        functools.partial(backward_kernel, chips),
        out_shape=jax.ShapeDtypeStruct((blocks, 2, 3 * d, LANES), BF16),
        in_specs=[HBM] * 8,
        out_specs=HBM,
        scratch_shapes=[
            vmem((tokens, d), BF16), vmem((d, tokens), BF16), vmem((tokens, d), BF16), vmem((d, tokens), BF16),
            vmem((tokens, d), BF16), vmem((2, d, BLOCK), BF16), vmem((2, d, BLOCK), BF16), vmem((2, BLOCK, d), BF16),
            vmem((d, ff), BF16), vmem((d, ff), BF16),
            vmem((tokens, BLOCK), BF16), vmem((per_layer, tokens, BLOCK), BF16), vmem((per_layer, tokens, BLOCK), BF16),
            vmem((2, 2, 3 * d, LANES), BF16), vmem((2, 3 * d, LANES), BF16), vmem((DEPTH, 3 * d, LANES), F32),
            vmem((blocks, chips + 1, chunk, LANES), BF16),
            sem((9,)), sem((2, 3)), sem((2,)), sem((2,)), sem((blocks, chips - 1)), sem((blocks, chips - 1)),
            sem((blocks, chips - 1)), sem((blocks, chips - 1)), sem, sem, sem((blocks,)),
        ],
        compiler_params=pltpu.CompilerParams(collective_id=0, has_side_effects=True, vmem_limit_bytes=VMEM_LIMIT),
        cost_estimate=pl.CostEstimate(flops=flops, bytes_accessed=64 << 20, transcendentals=0),
    )(a, at, dy, dyt, h, wg, wu, wd)


def adamw_kernel(count, sums, *refs):
    ins, outs, (g_ref, factor_ref, sem) = refs[:9], refs[9:18], refs[18:]
    blocks, _, d3, _ = sums.shape
    d = d3 // 3
    b = pl.program_id(0)

    @pl.when(b == 0)
    def _():
        def load(i):
            return pltpu.make_async_copy(sums.at[i], g_ref.at[i], sem.at[i])

        def start(i, _):
            load(i).start()
            return 0

        def square(i, total):
            load(i).wait()

            def some(k, total):
                r = pl.ds(pl.multiple_of(k * LANES, LANES), LANES)
                for half in range(2):
                    g = g_ref[i, half, r].astype(F32).reshape(LANES // 8, 8, LANES)
                    total = total + jnp.sum(g * g, axis=0)
                return total

            return lax.fori_loop(0, d3 // LANES, some, total)

        lax.fori_loop(0, blocks, start, 0)
        total = lax.fori_loop(0, blocks, square, jnp.zeros((8, LANES), F32))
        total = jnp.sum(jnp.sum(total, axis=1, keepdims=True), axis=0, keepdims=True)
        factor = jnp.minimum(1.0, 0.5 * lax.rsqrt(total / count + 1e-30))
        factor_ref[...] = jnp.broadcast_to(factor, factor_ref.shape)

    factor = factor_ref[0:1, :]
    for place in range(3):
        w_ref, m_ref, v_ref = (ins[3 * kind + place] for kind in range(3))
        w_out, m_out, v_out = (outs[3 * kind + place] for kind in range(3))
        for half in range(2):
            for k in range(0, d, LANES):
                g = g_ref[b, half, place * d + k : place * d + k + LANES, :].astype(F32)
                if place < 2:
                    at = (0, slice(k, k + LANES), slice(half * LANES, (half + 1) * LANES))
                else:
                    g = g.T
                    at = (0, slice(half * LANES, (half + 1) * LANES), slice(k, k + LANES))
                g = g * factor
                m = 0.9 * m_ref[at] + 0.1 * g
                v = 0.95 * v_ref[at] + 0.05 * g * g
                w = w_ref[at].astype(F32)
                w_out[at] = (w - 0.02 * (m * lax.rsqrt(v + 1e-8) + 0.1 * w)).astype(BF16)
                m_out[at] = m
                v_out[at] = v


def adamw(sums, arrays):
    layers, d, ff = arrays[0].shape
    per_layer = ff // BLOCK
    blocks = layers * per_layer
    wide = pl.BlockSpec((1, d, BLOCK), lambda b: (layers - 1 - b // per_layer, 0, b % per_layer))
    tall = pl.BlockSpec((1, BLOCK, d), lambda b: (layers - 1 - b // per_layer, b % per_layer, 0))
    specs = [wide, wide, tall] * 3
    return pl.pallas_call(
        functools.partial(adamw_kernel, 3 * layers * d * ff),
        grid=(blocks,),
        in_specs=[HBM] + specs,
        out_specs=specs,
        out_shape=[jax.ShapeDtypeStruct(a.shape, a.dtype) for a in arrays],
        scratch_shapes=[
            pltpu.VMEM((blocks, 2, 3 * d, LANES), BF16),
            pltpu.VMEM((8, LANES), F32),
            pltpu.SemaphoreType.DMA((blocks,)),
        ],
        compiler_params=pltpu.CompilerParams(vmem_limit_bytes=VMEM_LIMIT),
    )(sums, *arrays)


def solution(mesh):
    chips = mesh.shape["dp"] // 2

    def step(x, dy, *arrays):
        x, dy = x[0], dy[0]
        wg, wu, wd = arrays[:3]
        h, a, at, dyt = forward(x, dy, wg, wu, wd)
        sums = backward(chips, a, at, dy, dyt, h, wg, wu, wd)
        return tuple(adamw(sums, arrays))

    return jax.shard_map(
        step,
        mesh=mesh,
        in_specs=(P(("rep", "dp"), None, None),) * 2 + (P(None, None, None),) * 9,
        out_specs=(P("rep", None, None),) * 9,
        check_vma=False,
    )
```

time: 342 us -> 288 us (0.84)
  Pallas kernels: 341 us -> 287 us
    pallas_call x1, Pallas kernels: 255 us -> 200 us  [backward(): pl.pallas_call(functools.partial(backward_kernel, chips), out_shape=jax.S...]
where the time goes in v2:
time: 288 us
  Pallas kernels  287 us (100%)
    pallas_call x1, Pallas kernels, backward(): pl.pallas_call(functools.partial(backward_kernel, chips), out_shape=jax.S...  200 us
    pallas_call x1, Pallas kernels, adamw(): pl.pallas_call(functools.partial(adamw_kernel, 3 * layers * d * ff), grid...  59.2 us
    pallas_call x1, Pallas kernels, forward(): pl.pallas_call(forward_kernel, grid=(tokens // rows,), in_specs=[tile, ti...  27.5 us

profile of v2, /device:TPU:21, one launch (start us, length us, event | category | flops | bytes accessed | tf_op | source)
XLA Modules:
  0.0 287.7 jit_solution(10184198709584256177)
XLA Ops:
  0.6 27.5 %shard_map.178 = (bf16[2048,640]{1,0:T(8,128)(2,1)}, bf16[2,2048,640]{2,1,0:T(8,128)(2,1)}, bf16[2,640,2048]{2,1,0:T(8,128)(2,1)}, bf16[640,2048]{1,0:T(8,128)(2,1)}) custom-call(bf16[2048,640]{1,0:T(8,128)(2,1)} %bitcast.2, bf16[2048,640]{1,0:T(8,128)(2,1)} %bitcast.3, bf16[2,640,2048]{2,1,0:T(8,128)(2,1)} %refs_0_.1, bf16[2,640,2048]{2,1,0:T(8,128)(2,1)} %refs_1_.1, ...), custom_call_target="tpu_custom_call" | custom-call | tf_op jit(solution)/shard_map/pallas_call | solution.py:59
  28.2 200.2 %shard_map.179.sums = bf16[16,2,1920,128]{3,2,1,0:T(8,128)(2,1)} custom-call(bf16[2,2048,640]{2,1,0:T(8,128)(2,1)} %get-tuple-element.13.a_hbm, bf16[2,640,2048]{2,1,0:T(8,128)(2,1)} %get-tuple-element.14.at_hbm, bf16[2048,640]{1,0:T(8,128)(2,1)} %bitcast.4, bf16[640,2048]{1,0:T(8,128)(2,1)} %get-tuple-element.15.dyt_hbm, ...), custom_call_target="tpu_custom_call" | custom-call | flops 75161927680 | bytes 67108864 | tf_op jit(solution)/shard_map/pallas_call | solution.py:387
  228.3 59.2 %shard_map.180 = (bf16[2,640,2048]{2,1,0:T(8,128)(2,1)}, bf16[2,640,2048]{2,1,0:T(8,128)(2,1)}, bf16[2,2048,640]{2,1,0:T(8,128)(2,1)}, f32[2,640,2048]{2,1,0:T(8...) custom-call(bf16[16,2,1920,128]{3,2,1,0:T(8,128)(2,1)} %shard_map.17, ...), custom_call_target="tpu_custom_call" | custom-call | tf_op jit(solution)/shard_map/pallas_call | solution.py:468

commit v3 on v2

--- a/solution.py
+++ b/solution.py
@@ -13,6 +13,7 @@
 BLOCK = 256
 LANES = 128
 ROWS = 256
+WIDE = 2
 VMEM_LIMIT = 67_000_000
 
 
@@ -79,7 +80,8 @@
     )(x, dy, wg, wu, wd)
 
 
-TICKS = 5
+PARTS = 4
+TICKS = PARTS + 1
 LAG = 4
 DEPTH = 4
 
@@ -87,7 +89,7 @@
 def backward_kernel(
     chips, a_hbm, at_hbm, dy_hbm, dyt_hbm, h_hbm, wg_hbm, wu_hbm, wd_hbm, sums,
     a_ref, at_ref, dy_ref, dyt_ref, h_ref, wg_ref, wu_ref, wd_ref, allg_ref, allu_ref, p_ref, dg_ref, du_ref,
-    own_ref, got_ref, both_ref, land_ref,
+    own_ref, got_ref, both_ref, land_ref, spread_ref,
     load_sem, w_sem, pair_send, pair_recv, rs_send, rs_recv, ag_send, ag_recv, share_send, share_recv, keep_sem,
 ):
     layers, tokens, d = a_hbm.shape
@@ -145,8 +147,7 @@
     loads[0].start()
     for copy in weights(0, 0):
         copy.start()
-    for copy in loads[1:7]:
-        copy.start()
+    loads[1].start()
 
     barrier = pltpu.get_barrier_semaphore()
     for peer in (partner, along(1), along(-1)):
@@ -172,20 +173,20 @@
             rs_send.at[b, sem], rs_recv.at[b, sem], along(way_of(b, side)), MESH,
         )
 
-    def ag_copy(src, b, c, side, hop):
-        sem = side * near + hop - 1
+    def ag_copy(src, b, side, hop):
+        place = side * near + hop - 1
         return pltpu.make_async_remote_copy(
-            src, sums.at[b, core, rows_of(c), :], ag_send.at[b, sem], ag_recv.at[b, sem], along(way_of(b, side)), MESH
+            src, spread_ref.at[b, place], ag_send.at[b, place], ag_recv.at[b, place], along(way_of(b, 1 - side)), MESH
         )
 
     def share_copy(src, b, c):
         return pltpu.make_async_remote_copy(src, sums.at[b, core, rows_of(c), :], share_send, share_recv, partner, MESH)
 
+    def keep_copy(src, b, c):
+        return pltpu.make_async_copy(src, sums.at[b, core, rows_of(c), :], keep_sem)
+
     def done(b):
         return land_ref.at[b, rs_place(0, near)]
-
-    def keep_copy(b):
-        return pltpu.make_async_copy(done(b), sums.at[b, core, rows_of(z), :], keep_sem.at[b])
 
     def scatter_step(b, s):
         four = lax.rem(b, DEPTH)
@@ -230,36 +231,35 @@
         @pl.when(s == near + 1)
         def _():
             for side in range(2):
-                ag_copy(done(b), b, z, side, 1).start()
+                ag_copy(done(b), b, side, 1).start()
             share_copy(done(b), b, z).start()
-            keep_copy(b).start()
+            keep_copy(done(b), b, z).start()
 
     def gather_step(b, hop):
         for side, reach in ((0, near), (1, far)):
 
             @pl.when(hop <= reach)
             def _(side=side, reach=reach):
-                c = wrap(z - way_of(b, side) * hop)
-                here = sums.at[b, core, rows_of(c), :]
-                ag_copy(here, b, c, side, hop).wait_recv()
+                c = wrap(z - way_of(b, 1 - side) * hop)
+                here = spread_ref.at[b, side * near + hop - 1]
+                ag_copy(here, b, side, hop).wait_recv()
 
                 @pl.when(hop < reach)
                 def _():
-                    ag_copy(here, b, c, side, hop + 1).start()
+                    ag_copy(here, b, side, hop + 1).start()
 
                 share_copy(here, b, c).start()
+                keep_copy(here, b, c).start()
 
     def tick(now):
         first = lax.rem(inverse * now, TICKS)
-        for p, step in ((first, scatter_step), (first + TICKS, gather_step)):
+        later = jnp.where(first > near, first, first + TICKS)
+        for p, step, phase in ((later, gather_step, later - near), (first, scatter_step, first + 1)):
             t = (now - LAG * p + 16 * TICKS) // TICKS - 17
-            ok = is_block(t)
-            if step is gather_step:
-                ok = ok & (p < near + 1 + near)
-
-            @pl.when(ok)
-            def _(t=t, step=step):
-                step(block_of(t), first + 1)
+
+            @pl.when(is_block(t) & (phase <= (near + 1 if step is scatter_step else near)))
+            def _(t=t, step=step, phase=phase):
+                step(block_of(t), phase)
 
     def token_tiles(slot, kept, first, count):
         for i in range(count):
@@ -291,7 +291,7 @@
             dy_ref[r] = by_h
             dyt_ref[:, r] = by_h.T
 
-    parts = TICKS - 1
+    parts = PARTS
     each = tiles // parts
 
     def slot_of_work(t, _):
@@ -310,6 +310,13 @@
             def _():
                 loads[0].wait()
                 loads[1].wait()
+                loads[2].start()
+                loads[3].start()
+
+            @pl.when(t == 1)
+            def _():
+                for copy in loads[4:7]:
+                    copy.start()
 
             for copy in weights(b, slot):
                 copy.wait()
@@ -333,7 +340,7 @@
                 for half in range(2):
                     own_ref[slot, half, place * d : (place + 1) * d, :] = g[:, half * LANES : (half + 1) * LANES]
             pair_copy(b).start()
-            tick(TICKS * t + parts)
+            tick(TICKS * t + TICKS - 1)
 
         @pl.when(jnp.logical_not(is_block(t)))
         def _():
@@ -348,7 +355,8 @@
                 return 0
 
             lax.fori_loop(0, parts, part, 0)
-            tick(TICKS * t + parts)
+            for i in range(parts, TICKS):
+                tick(TICKS * t + i)
             for copy in loads[7:]:
                 copy.wait()
 
@@ -366,11 +374,11 @@
         for side, reach in ((0, near), (1, far)):
             for hop in range(1, reach + 1):
                 rs_copy(b, side, hop).wait_send()
-                ag_copy(done(b), b, z, side, hop).wait_send()
-        keep_copy(b).wait()
+                ag_copy(done(b), b, side, hop).wait_send()
         return 0
 
     lax.fori_loop(0, blocks, finish, 0)
+    pltpu.make_async_copy(sums.at[:, core], sums.at[:, core], keep_sem).wait()
     pltpu.make_async_copy(sums.at[:, core], sums.at[:, core], share_send).wait()
     pltpu.make_async_copy(sums.at[:, other], sums.at[:, other], share_recv).wait()
 
@@ -395,9 +403,9 @@
             vmem((d, ff), BF16), vmem((d, ff), BF16),
             vmem((tokens, BLOCK), BF16), vmem((per_layer, tokens, BLOCK), BF16), vmem((per_layer, tokens, BLOCK), BF16),
             vmem((2, 2, 3 * d, LANES), BF16), vmem((2, 3 * d, LANES), BF16), vmem((DEPTH, 3 * d, LANES), F32),
-            vmem((blocks, chips + 1, chunk, LANES), BF16),
+            vmem((blocks, chips + 1, chunk, LANES), BF16), vmem((blocks, chips - 1, chunk, LANES), BF16),
             sem((9,)), sem((2, 3)), sem((2,)), sem((2,)), sem((blocks, chips - 1)), sem((blocks, chips - 1)),
-            sem((blocks, chips - 1)), sem((blocks, chips - 1)), sem, sem, sem((blocks,)),
+            sem((blocks, chips - 1)), sem((blocks, chips - 1)), sem, sem, sem,
         ],
         compiler_params=pltpu.CompilerParams(collective_id=0, has_side_effects=True, vmem_limit_bytes=VMEM_LIMIT),
         cost_estimate=pl.CostEstimate(flops=flops, bytes_accessed=64 << 20, transcendentals=0),
@@ -408,9 +416,9 @@
     ins, outs, (g_ref, factor_ref, sem) = refs[:9], refs[9:18], refs[18:]
     blocks, _, d3, _ = sums.shape
     d = d3 // 3
-    b = pl.program_id(0)
-
-    @pl.when(b == 0)
+    step = pl.program_id(0)
+
+    @pl.when(step == 0)
     def _():
         def load(i):
             return pltpu.make_async_copy(sums.at[i], g_ref.at[i], sem.at[i])
@@ -438,17 +446,19 @@
         factor_ref[...] = jnp.broadcast_to(factor, factor_ref.shape)
 
     factor = factor_ref[0:1, :]
-    for place in range(3):
-        w_ref, m_ref, v_ref = (ins[3 * kind + place] for kind in range(3))
-        w_out, m_out, v_out = (outs[3 * kind + place] for kind in range(3))
-        for half in range(2):
+    for sub in range(2 * WIDE):
+        start, half = sub * LANES, sub % 2
+        block = step * WIDE + sub // 2
+        for place in range(3):
+            w_ref, m_ref, v_ref = (ins[3 * kind + place] for kind in range(3))
+            w_out, m_out, v_out = (outs[3 * kind + place] for kind in range(3))
             for k in range(0, d, LANES):
-                g = g_ref[b, half, place * d + k : place * d + k + LANES, :].astype(F32)
+                g = g_ref[block, half, place * d + k : place * d + k + LANES, :].astype(F32)
                 if place < 2:
-                    at = (0, slice(k, k + LANES), slice(half * LANES, (half + 1) * LANES))
+                    at = (0, slice(k, k + LANES), slice(start, start + LANES))
                 else:
                     g = g.T
-                    at = (0, slice(half * LANES, (half + 1) * LANES), slice(k, k + LANES))
+                    at = (0, slice(start, start + LANES), slice(k, k + LANES))
                 g = g * factor
                 m = 0.9 * m_ref[at] + 0.1 * g
                 v = 0.95 * v_ref[at] + 0.05 * g * g
@@ -462,12 +472,13 @@
     layers, d, ff = arrays[0].shape
     per_layer = ff // BLOCK
     blocks = layers * per_layer
-    wide = pl.BlockSpec((1, d, BLOCK), lambda b: (layers - 1 - b // per_layer, 0, b % per_layer))
-    tall = pl.BlockSpec((1, BLOCK, d), lambda b: (layers - 1 - b // per_layer, b % per_layer, 0))
+    steps = per_layer // WIDE
+    wide = pl.BlockSpec((1, d, WIDE * BLOCK), lambda i: (layers - 1 - i // steps, 0, i % steps))
+    tall = pl.BlockSpec((1, WIDE * BLOCK, d), lambda i: (layers - 1 - i // steps, i % steps, 0))
     specs = [wide, wide, tall] * 3
     return pl.pallas_call(
         functools.partial(adamw_kernel, 3 * layers * d * ff),
-        grid=(blocks,),
+        grid=(layers * steps,),
         in_specs=[HBM] + specs,
         out_specs=specs,
         out_shape=[jax.ShapeDtypeStruct(a.shape, a.dtype) for a in arrays],

time: 288 us -> 286 us (level)
    pallas_call x1, Pallas kernels: 200 us -> 197 us  [backward(): pl.pallas_call(functools.partial(backward_kernel, chips), out_shape=jax.S...]
where the time goes in v3:
time: 286 us; the launch traced here: 285 us
  Pallas kernels  285 us (100%)
    pallas_call x1, Pallas kernels, backward(): pl.pallas_call(functools.partial(backward_kernel, chips), out_shape=jax.S...  197 us
    pallas_call x1, Pallas kernels, adamw(): pl.pallas_call(functools.partial(adamw_kernel, 3 * layers * d * ff), grid...  60.2 us
    pallas_call x1, Pallas kernels, forward(): pl.pallas_call(forward_kernel, grid=(tokens // rows,), in_specs=[tile, ti...  27.5 us

profile of v3, /device:TPU:21, one launch (start us, length us, event | category | flops | bytes accessed | tf_op | source)
XLA Modules:
  0.0 285.4 jit_solution(16186051207718177526)
XLA Ops:
  0.6 27.5 %shard_map.178 = (bf16[2048,640]{1,0:T(8,128)(2,1)}, bf16[2,2048,640]{2,1,0:T(8,128)(2,1)}, bf16[2,640,2048]{2,1,0:T(8,128)(2,1)}, bf16[640,2048]{1,0:T(8,128)(2,1)}) custom-call(bf16[2048,640]{1,0:T(8,128)(2,1)} %bitcast.2, bf16[2048,640]{1,0:T(8,128)(2,1)} %bitcast.3, bf16[2,640,2048]{2,1,0:T(8,128)(2,1)} %refs_0_.1, bf16[2,640,2048]{2,1,0:T(8,128)(2,1)} %refs_1_.1, ...), custom_call_target="tpu_custom_call" | custom-call | tf_op jit(solution)/shard_map/pallas_call | solution.py:60
  28.2 196.9 %shard_map.179.sums = bf16[16,2,1920,128]{3,2,1,0:T(8,128)(2,1)} custom-call(bf16[2,2048,640]{2,1,0:T(8,128)(2,1)} %get-tuple-element.13.a_hbm, bf16[2,640,2048]{2,1,0:T(8,128)(2,1)} %get-tuple-element.14.at_hbm, bf16[2048,640]{1,0:T(8,128)(2,1)} %bitcast.4, bf16[640,2048]{1,0:T(8,128)(2,1)} %get-tuple-element.15.dyt_hbm, ...), custom_call_target="tpu_custom_call" | custom-call | flops 75161927680 | bytes 67108864 | tf_op jit(solution)/shard_map/pallas_call | solution.py:395
  225.1 60.2 %shard_map.180 = (bf16[2,640,2048]{2,1,0:T(8,128)(2,1)}, bf16[2,640,2048]{2,1,0:T(8,128)(2,1)}, bf16[2,2048,640]{2,1,0:T(8,128)(2,1)}, f32[2,640,2048]{2,1,0:T(8...) custom-call(bf16[16,2,1920,128]{3,2,1,0:T(8,128)(2,1)} %shard_map.17, ...), custom_call_target="tpu_custom_call" | custom-call | tf_op jit(solution)/shard_map/pallas_call | solution.py:479
